TPU v7x, 32 devices: a whole 2x2x4 slice. The times are simulated.
32 devices in a mesh: row: 4 (over y, x), col: 8 (over z, core).
Axes of the slice: x: 2, y: 2, z: 4, core: 2. Of those that a mesh axis runs over, the one named last changes fastest.
Arguments:
- values: bfloat16 [4096, 4096], P('row', 'col'), may hold values from 0.0001296997 to 0.12988281
- tile_mask: int32 [32, 32], P('row', 'col'), may hold values 0 or 1
- keep_mask: int32 [32, 32], P('row', 'col'), may hold values 0 or 1
- thr_index: int32 [4096], P('col'), may hold values from 0 to 9
Outputs:
- expanded: bfloat16 [4096, 4096], P('row', 'col')
All inputs are finite; a program needn't handle non-finite values. No bound on the sum of `tile_mask` or of `keep_mask` on one device may be relied on, other than what follows from the above.
Results may differ from a plain program's by a relative error of at most 0.0004.
Values may be sent and summed in bfloat16 or wider, within the bound.
No kernel may reach another device: no remote copies, remote signals or barrier semaphores. Data moves between devices by JAX's collectives and lax.ppermute only.
A program may use at most 64 MiB of HBM per device.

v0:
```python
import jax
import jax.numpy as jnp
from jax import lax
from jax.sharding import PartitionSpec as P

TB = 128


def on_device(values, tile_mask, keep_mask, thr_index):
    row_count, col_count = values.shape
    row_tiles = row_count // TB
    col_tiles = col_count // TB
    matrix = (
        values.reshape(row_tiles, TB, col_tiles, TB)
        * tile_mask[:, None, :, None].astype(jnp.bfloat16)
    ).reshape(row_count, col_count)
    kept_cells = jnp.broadcast_to(
        keep_mask[:, None, :, None].astype(jnp.float32), (row_tiles, TB, col_tiles, TB)
    ).reshape(row_count, col_count)
    order_all = row_count * lax.axis_size("row")
    thresholds = 0.125 * thr_index.astype(jnp.float32)
    col_panel = lax.all_gather(matrix, "row", axis=0, tiled=True)
    product = jnp.dot(
        lax.all_gather(matrix, "col", axis=1, tiled=True),
        col_panel,
        preferred_element_type=jnp.float32,
    )
    outputs = []
    for phase_idx in range(col_tiles):
        lo_col = phase_idx * TB
        part_prod = product[:, lo_col : lo_col + TB]
        col_means = lax.psum(jnp.sum(part_prod, axis=0), "row") / order_all
        pruned = (
            jnp.maximum(part_prod - thresholds[lo_col : lo_col + TB] * col_means, 0.0)
            * kept_cells[:, lo_col : lo_col + TB]
        )
        col_totals = lax.psum(jnp.sum(pruned, axis=0), "row") / order_all
        outputs.append(pruned / jnp.maximum(col_totals, 0.1))
    result = jnp.concatenate(outputs, axis=1)
    return result.astype(jnp.bfloat16)


def solution(mesh):
    return jax.shard_map(
        on_device,
        mesh=mesh,
        in_specs=(P("row", "col"), P("row", "col"), P("row", "col"), P("col")),
        out_specs=P("row", "col"),
        check_vma=False,
    )
```

profile of v0, /device:TPU:0, one launch (start us, length us, event | category | flops | bytes accessed | tf_op | source)
XLA Modules:
  0.0 188.3 jit_solution(8773886451617511830)
XLA Ops:
  6.5 0.0 all-gather.5.cloned.1.call-start
  6.5 0.7 convert_element_type.12
  7.2 0.1 copy.5
  7.3 0.3 mul.41
  7.7 0.0 copy-start.1
  7.7 2.3 %bitcast_multiply_fusion = bf16[1024,512]{1,0:T(8,128)(2,1)} fusion(bf16[1024,512]{1,0:T(8,128)(2,1)} %param.4, bf16[128,8,4,128]{3,2,1,0:T(4,128)(2,1)S(1)} %bitcast.14), kind=kLoop, calls=%fused_computation.1 | loop fusion | flops 524288 | bytes 3145728 | tf_op jit(solution)/shard_map/mul | solution.py:14
  10.0 0.0 all-gather.5.cloned.1.call-update
  10.0 0.0 all-gather.3.cloned.1.call-start
  10.1 0.7 all-gather.3.cloned.1.call-update
  10.8 0.1 copy.6
  10.9 0.3 broadcast_in_dim.2
  11.2 0.0 copy-start.2
  11.3 0.2 copy.11
  11.4 0.5 copy-done.2
  11.9 53.6 %all-gather.5.cloned.1.call-done = bf16[4096,512]{1,0:T(8,128)(2,1)} async-done(((bf16[1024,512]{1,0:T(8,128)(2,1)}), bf16[4096,512]{1,0:T(8,128)(2,1)}) %all-gather.5.cloned.1.call-update) | async-done | bytes 4194320 | tf_op jit(solution)/shard_map/all_gather | solution.py:22
  65.5 83.7 %all-gather.3.cloned.1.call-done = bf16[1024,4096]{1,0:T(8,128)(2,1)} async-done(((bf16[1024,512]{1,0:T(8,128)(2,1)}), bf16[1024,4096]{1,0:T(8,128)(2,1)}) %all-gather.3.cloned.1.call-update) | async-done | bytes 8388624 | tf_op jit(solution)/shard_map/all_gather | solution.py:24
  149.2 8.1 %fusion.4 = f32[1024,512]{1,0:T(8,128)S(1)} fusion(bf16[1024,4096]{1,0:T(8,128)(2,1)} %all-gather.3.cloned.1.call-done, bf16[4096,512]{1,0:T(8,128)(2,1)} %all-gather.5.cloned.1.call-done), kind=kOutput, calls=%fused_computation.28 | convolution fusion | flops 4294967296 | bytes 14680064 | tf_op jit(solution)/shard_map/dot_general | solution.py:23
  157.3 1.3 copy-done
  158.7 0.2 slice_reduce_fusion.3
  158.8 9.8 %all-reduce.1 = (f32[128]{0:T(128)S(1)}, f32[128]{0:T(128)S(1)}, f32[128]{0:T(128)S(1)}, f32[128]{0:T(128)S(1)}) all-reduce(f32[128]{0:T(128)S(1)} %get-tuple-element.9, f32[128]{0:T(128)S(1)} %get-tuple-element.10, f32[128]{0:T(128)S(1)} %get-tuple-element.11, f32[128]{0:T(128)S(1)} %get-tuple-element.12), channel_id=1, replica_groups=mesh['row'=4,'col'=8] {'row'}, use_global_device_ids=true, to_apply=%region_1.0 | all-reduce | flops 512 | bytes 4096 | tf_op jit(solution)/shard_map/psum | solution.py:32
  168.7 1.8 fusion
  170.5 8.0 %all-reduce = (f32[128]{0:T(128)S(1)}, f32[128]{0:T(128)S(1)}, f32[128]{0:T(128)S(1)}, f32[128]{0:T(128)S(1)}) all-reduce(f32[128]{0:T(128)S(1)} %get-tuple-element.6, f32[128]{0:T(128)S(1)} %get-tuple-element.7, f32[128]{0:T(128)S(1)} %get-tuple-element.8, f32[128]{0:T(128)S(1)} %get-tuple-element.5), channel_id=1, replica_groups=mesh['row'=4,'col'=8] {'row'}, use_global_device_ids=true, to_apply=%region_15.0 | all-reduce | flops 512 | bytes 4096 | tf_op jit(solution)/shard_map/psum | solution.py:37
  178.5 1.9 %divide_convert_fusion.3 = (bf16[1024,128]{1,0:T(8,128)(2,1)S(1)}, bf16[1024,128]{1,0:T(8,128)(2,1)S(1)}, bf16[1024,128]{1,0:T(8,128)(2,1)S(1)}, bf16[1024,128]{1,0:T(8,128)(2,1)S(1)}) fusion(f32[128]{0:T(128)S(1)} %get-tuple-element.32, f32[1024,512]{1,0:T(8,128)S(1)} %bitcast.12, f32[128]{0:T(128)S(1)} %get-tuple-element.28, f32[1024,512]{1,0:T(8,128)} %copy-done, ...), kind=kLoop, calls=%fused_computation.10 | loop fusion | flops 2621440 | bytes 5246976 | tf_op jit(solution)/shard_map/convert
  180.4 1.1 pad_maximum_fusion
  (7 shorter events, 0.0 us)
Async XLA Ops:
  6.5 59.0 %all-gather.5.cloned.1.call-start = ((), (), s32[]{:S(2)}) async-start(), calls=%async_computation.1 | async-start | bytes 5242880 | tf_op jit(solution)/shard_map/all_gather | solution.py:22
  7.7 3.1 %copy-start.1 = (s32[8,4]{0,1:T(4,128)S(1)}, s32[8,4]{0,1:T(4,128)}, u32[]{:S(2)}) copy-start(s32[8,4]{0,1:T(4,128)} %param.6) | copy-start | bytes 388
  10.0 139.1 %all-gather.3.cloned.1.call-start = ((), (), s32[]{:S(2)}) async-start(), calls=%async_computation | async-start | bytes 9437184 | tf_op jit(solution)/shard_map/all_gather | solution.py:24
  11.2 0.7 copy-start.2
  157.3 1.4 copy-start
Sparse Core Ops, SparseCore 0:
  10.2 55.2 all-gather.4
  67.1 82.0 all-gather.2
where the time goes:
time: 189 us; the launch traced here: 188 us
  waiting for transfers between devices  138 us (73%)
  blocking collectives  17.8 us (9%)
  between operations  13.5 us (7%)
  matrix products  8.14 us (4%)
  other arithmetic  8.02 us (4%)
  local copies, waits for them, and re-layouts  2.87 us (2%)
    all_gather x1, waiting for transfers between devices, on_device(): lax.all_gather(matrix, 'col', axis=1, tiled=True)  83.7 us
    all_gather x1, waiting for transfers between devices, on_device(): col_panel = lax.all_gather(matrix, 'row', axis=0, tiled=True)  53.6 us
    psum x1, blocking collectives, on_device(): col_means = lax.psum(jnp.sum(part_prod, axis=0), 'row') / order_all  9.85 us
    dot_general x1, matrix products, on_device(): jnp.dot(lax.all_gather(matrix, 'col', axis=1, tiled=True), col_panel, pre...  8.14 us
    psum x1, blocking collectives, on_device(): col_totals = lax.psum(jnp.sum(pruned, axis=0), 'row') / order_all  7.98 us
  transfers between devices with their start and end apart: 2, of which 2 were waited for; matrix products, arithmetic and copies ran while one was open for 0% of the time, Pallas kernels for 0%

commit v1 on v0

--- a/solution.py
+++ b/solution.py
@@ -1,9 +1,25 @@
+import functools
 import jax
 import jax.numpy as jnp
 from jax import lax
 from jax.sharding import PartitionSpec as P
 
 TB = 128
+
+
+def _begin_sheet(base_x, array_axis):
+    n = jax.lax.axis_size("row")
+    pile = [base_x]
+    for dev_i in [*range(n - 1)]:
+        w_next = jax.lax.ppermute(pile[-1], "row", [(dev, (dev + 1) % n) for dev in range(n)])
+        pile.append(w_next)
+    x_next = jnp.concatenate(pile[::-1], axis=array_axis)
+    y = jax.lax.axis_index("row")
+    v1 = jnp.roll(x_next, (y + 1) * base_x.shape[array_axis], axis=array_axis)
+    return v1
+
+
+remake_results = functools.partial(_begin_sheet, array_axis=0)
 
 
 def on_device(values, tile_mask, keep_mask, thr_index):
@@ -19,7 +35,7 @@
     ).reshape(row_count, col_count)
     order_all = row_count * lax.axis_size("row")
     thresholds = 0.125 * thr_index.astype(jnp.float32)
-    col_panel = lax.all_gather(matrix, "row", axis=0, tiled=True)
+    col_panel = remake_results(matrix)
     product = jnp.dot(
         lax.all_gather(matrix, "col", axis=1, tiled=True),
         col_panel,

time: 189 us -> 143 us (0.76)
  waiting for transfers between devices: 138 us -> 72.4 us
  local copies, waits for them, and re-layouts: 2.87 us -> 18.1 us
  starting transfers between devices: 0.04 us -> 3.81 us
    all_gather x1, waiting for transfers between devices: 83.7 us -> 0.01 us  [on_device(): lax.all_gather(matrix, 'col', axis=1, tiled=True)]
    ppermute x0 -> x3, waiting for transfers between devices: none -> 72.4 us  [_begin_sheet(): jax.lax.ppermute(pile[-1], 'row', [(dev, (dev + 1) % n) for dev in range(...]
    all_gather x1 -> x0, waiting for transfers between devices: 53.6 us -> none  [on_device(): col_panel = lax.all_gather(matrix, 'row', axis=0, tiled=True)]
    unnamed x7 -> x18, local copies, waits for them, and re-layouts: 2.02 us -> 16.2 us
    ppermute x0 -> x3, starting transfers between devices: none -> 3.81 us  [_begin_sheet(): jax.lax.ppermute(pile[-1], 'row', [(dev, (dev + 1) % n) for dev in range(...]
    psum x1, blocking collectives: 9.85 us -> 7.47 us  [on_device(): col_means = lax.psum(jnp.sum(part_prod, axis=0), 'row') / order_all]
    psum x1, blocking collectives: 7.98 us -> 9.99 us  [on_device(): col_totals = lax.psum(jnp.sum(pruned, axis=0), 'row') / order_all]
  transfers between devices with their start and end apart: 2 -> 4, of which waited for: 2 -> 3; matrix products, arithmetic and copies ran while one was open for 0% -> 11% of each run, Pallas kernels for 0% -> 0%
where the time goes in v1:
time: 143 us; the launch traced here: 142 us
  waiting for transfers between devices  72.4 us (51%)
  local copies, waits for them, and re-layouts  18.1 us (13%)
  blocking collectives  17.5 us (12%)
  between operations  13.5 us (9%)
  other arithmetic  8.71 us (6%)
  matrix products  8.14 us (6%)
  starting transfers between devices  3.81 us (3%)
    ppermute x3, waiting for transfers between devices, _begin_sheet(): jax.lax.ppermute(pile[-1], 'row', [(dev, (dev + 1) % n) for dev in range(...  72.4 us
    unnamed x18, local copies, waits for them, and re-layouts  16.2 us
    psum x1, blocking collectives, on_device(): col_totals = lax.psum(jnp.sum(pruned, axis=0), 'row') / order_all  9.99 us
    dot_general x1, matrix products, on_device(): jnp.dot(lax.all_gather(matrix, 'col', axis=1, tiled=True), col_panel, pre...  8.14 us
    psum x1, blocking collectives, on_device(): col_means = lax.psum(jnp.sum(part_prod, axis=0), 'row') / order_all  7.47 us
    ppermute x3, starting transfers between devices, _begin_sheet(): jax.lax.ppermute(pile[-1], 'row', [(dev, (dev + 1) % n) for dev in range(...  3.81 us
  transfers between devices with their start and end apart: 4, of which 3 were waited for; matrix products, arithmetic and copies ran while one was open for 11% of the time, Pallas kernels for 0%

profile of v1, /device:TPU:0, one launch (start us, length us, event | category | flops | bytes accessed | tf_op | source)
XLA Modules:
  0.0 142.1 jit_solution(16810162328017821033)
XLA Ops:
  6.5 0.7 convert_element_type.12
  7.7 2.3 %bitcast_multiply_fusion = bf16[1024,512]{1,0:T(8,128)(2,1)} fusion(bf16[1024,512]{1,0:T(8,128)(2,1)} %param.4, bf16[128,8,4,128]{3,2,1,0:T(4,128)(2,1)S(1)} %bitcast.13), kind=kLoop, calls=%fused_computation.3 | loop fusion | flops 524288 | bytes 3145728 | tf_op jit(solution)/shard_map/mul | solution.py:30
  10.0 3.0 %collective-permute-start = (bf16[1024,512]{1,0:T(8,128)(2,1)}, bf16[1024,512]{1,0:T(8,128)(2,1)S(1)}, u32[]{:S(2)}, u32[]{:S(2)}) collective-permute-start(bf16[1024,512]{1,0:T(8,128)(2,1)} %bitcast_multiply_fusion), channel_id=1, source_target_pairs={{0,8},{8,16},{16,24},{24,0},{1,9},{9,17},{17,25},{25,1},{2,10},{10... | collective-permute-start | bytes 3145736 | tf_op jit(solution)/shard_map/ppermute | solution.py:14
  13.1 24.3 %collective-permute-done = bf16[1024,512]{1,0:T(8,128)(2,1)S(1)} collective-permute-done((bf16[1024,512]{1,0:T(8,128)(2,1)}, bf16[1024,512]{1,0:T(8,128)(2,1)S(1)}, u32[]{:S(2)}, u32[]{:S(2)}) %collective-permute-start) | collective-permute-done | bytes 1048608 | tf_op jit(solution)/shard_map/ppermute | solution.py:14
  37.4 1.0 copy-done.2
  38.4 0.8 collective-permute-start.1
  39.2 24.6 %collective-permute-done.1 = bf16[1024,512]{1,0:T(8,128)(2,1)} collective-permute-done((bf16[1024,512]{1,0:T(8,128)(2,1)S(1)}, bf16[1024,512]{1,0:T(8,128)(2,1)}, u32[]{:S(2)}, u32[]{:S(2)}) %collective-permute-start.1) | collective-permute-done | bytes 1048608 | tf_op jit(solution)/shard_map/ppermute | solution.py:14
  63.8 0.7 convert_element_type.14
  65.2 23.5 %collective-permute-done.2 = bf16[1024,512]{1,0:T(8,128)(2,1)} collective-permute-done((bf16[1024,512]{1,0:T(8,128)(2,1)}, bf16[1024,512]{1,0:T(8,128)(2,1)}, u32[]{:S(2)}, u32[]{:S(2)}) %collective-permute-start.2) | collective-permute-done | bytes 1048608 | tf_op jit(solution)/shard_map/ppermute | solution.py:14
  88.6 2.4 %constant_dynamic-update-slice_fusion.7 = bf16[8192,512]{1,0:T(8,128)(2,1)} fusion(bf16[1024,512]{1,0:T(8,128)(2,1)} %collective-permute-done.2), kind=kLoop, calls=%fused_computation.28 | loop fusion | bytes 2097152
  91.0 2.3 %constant_dynamic-update-slice_fusion.6 = bf16[8192,512]{1,0:T(8,128)(2,1)} fusion(bf16[8192,512]{1,0:T(8,128)(2,1)} %constant_dynamic-update-slice_fusion.7, bf16[1024,512]{1,0:T(8,128)(2,1)} %collective-permute-done.1), kind=kLoop, calls=%fused_computation.27 | loop fusion | bytes 2097152
  93.3 2.3 %constant_dynamic-update-slice_fusion.5 = bf16[8192,512]{1,0:T(8,128)(2,1)} fusion(bf16[8192,512]{1,0:T(8,128)(2,1)} %constant_dynamic-update-slice_fusion.6, bf16[1024,512]{1,0:T(8,128)(2,1)} %copy-done.2), kind=kLoop, calls=%fused_computation.26 | loop fusion | bytes 2097152
  95.6 1.0 constant_dynamic-update-slice_fusion.4
  96.6 2.3 %constant_dynamic-update-slice_fusion.3 = bf16[8192,512]{1,0:T(8,128)(2,1)} fusion(bf16[8192,512]{1,0:T(8,128)(2,1)} %constant_dynamic-update-slice_fusion.4, bf16[1024,512]{1,0:T(8,128)(2,1)} %collective-permute-done.2), kind=kLoop, calls=%fused_computation.24 | loop fusion | bytes 2097152
  98.9 2.3 %constant_dynamic-update-slice_fusion.2 = bf16[8192,512]{1,0:T(8,128)(2,1)} fusion(bf16[8192,512]{1,0:T(8,128)(2,1)} %constant_dynamic-update-slice_fusion.3, bf16[1024,512]{1,0:T(8,128)(2,1)} %collective-permute-done.1), kind=kLoop, calls=%fused_computation.23 | loop fusion | bytes 2097152
  101.2 1.0 constant_dynamic-update-slice_fusion.1
  102.2 1.1 constant_dynamic-update-slice_fusion
  103.3 8.1 %fusion = f32[1024,512]{1,0:T(8,128)S(1)} fusion(bf16[1024,4096]{1,0:T(8,128)(2,1)} %all-gather.2.cloned.1.call-done, bf16[8192,512]{1,0:T(8,128)(2,1)} %constant_dynamic-update-slice_fusion, s32[]{:T(128)S(6)} %select_n.14), kind=kOutput, calls=%fused_computation | convolution fusion | flops 4294967296 | bytes 14680068 | tf_op jit(solution)/shard_map/dot_general | solution.py:39
  111.5 1.3 copy-done
  113.0 7.5 %all-reduce.1 = (f32[128]{0:T(128)S(1)}, f32[128]{0:T(128)S(1)}, f32[128]{0:T(128)S(1)}, f32[128]{0:T(128)S(1)}) all-reduce(f32[128]{0:T(128)S(1)} %get-tuple-element.9, f32[128]{0:T(128)S(1)} %get-tuple-element.10, f32[128]{0:T(128)S(1)} %get-tuple-element.11, f32[128]{0:T(128)S(1)} %get-tuple-element.12), channel_id=1, replica_groups=mesh['row'=4,'col'=8] {'row'}, use_global_device_ids=true, to_apply=%region_1.2 | all-reduce | flops 512 | bytes 4096 | tf_op jit(solution)/shard_map/psum | solution.py:48
  120.4 1.8 %fusion.2 = (f32[128]{0:T(128)S(1)}, f32[128]{0:T(128)S(1)}, f32[128]{0:T(128)S(1)}, f32[128]{0:T(128)S(1)}) fusion(f32[1024,512]{1,0:T(8,128)S(1)} %bitcast.10, f32[128]{0:T(128)S(1)} %get-tuple-element.28, f32[1024,512]{1,0:T(8,128)} %copy-done, f32[128]{0:T(128)S(1)} %get-tuple-element.26, f32[128]{0:T(128)S(1)} %get-tuple-element.27, ...), kind=kLoop, calls=%fused_computation.17 | loop fusion | flops 2096640 | bytes 4198400 | tf_op jit(solution)/shard_map/reduce_sum | solution.py:53
  122.3 10.0 %all-reduce = (f32[128]{0:T(128)S(1)}, f32[128]{0:T(128)S(1)}, f32[128]{0:T(128)S(1)}, f32[128]{0:T(128)S(1)}) all-reduce(f32[128]{0:T(128)S(1)} %get-tuple-element.6, f32[128]{0:T(128)S(1)} %get-tuple-element.7, f32[128]{0:T(128)S(1)} %get-tuple-element.8, f32[128]{0:T(128)S(1)} %get-tuple-element.5), channel_id=1, replica_groups=mesh['row'=4,'col'=8] {'row'}, use_global_device_ids=true, to_apply=%region_15.16 | all-reduce | flops 512 | bytes 4096 | tf_op jit(solution)/shard_map/psum | solution.py:53
  132.3 1.9 %divide_convert_fusion.3 = (bf16[1024,128]{1,0:T(8,128)(2,1)S(1)}, bf16[1024,128]{1,0:T(8,128)(2,1)S(1)}, bf16[1024,128]{1,0:T(8,128)(2,1)S(1)}, bf16[1024,128]{1,0:T(8,128)(2,1)S(1)}) fusion(f32[128]{0:T(128)S(1)} %get-tuple-element.32, f32[1024,512]{1,0:T(8,128)S(1)} %bitcast.11, f32[128]{0:T(128)S(1)} %get-tuple-element.28, f32[1024,512]{1,0:T(8,128)} %copy-done, ...), kind=kLoop, calls=%fused_computation.12 | loop fusion | flops 2621440 | bytes 5246976 | tf_op jit(solution)/shard_map/convert
  134.2 1.1 pad_maximum_fusion
  (22 shorter events, 1.2 us)
Async XLA Ops:
  6.5 58.6 %copy-start.4 = (s32[512]{0:T(512)S(1)}, s32[512]{0:T(512)}, u32[]{:S(2)}) copy-start(s32[512]{0:T(512)} %param.7) | copy-start | bytes 6148
  6.5 96.8 %all-gather.2.cloned.1.call-start = ((), (), s32[]{:S(2)}) async-start(), calls=%async_computation | async-start | bytes 9437184 | tf_op jit(solution)/shard_map/all_gather | solution.py:40
  10.0 85.5 %copy-start.1 = (bf16[1024,512]{1,0:T(8,128)(2,1)S(1)}, bf16[1024,512]{1,0:T(8,128)(2,1)}, u32[]{:S(2)}) copy-start(bf16[1024,512]{1,0:T(8,128)(2,1)} %bitcast_multiply_fusion) | copy-start | bytes 3145732
  10.0 27.3 %collective-permute-start = (bf16[1024,512]{1,0:T(8,128)(2,1)}, bf16[1024,512]{1,0:T(8,128)(2,1)S(1)}, u32[]{:S(2)}, u32[]{:S(2)}) collective-permute-start(bf16[1024,512]{1,0:T(8,128)(2,1)} %bitcast_multiply_fusion), channel_id=1, source_target_pairs={{0,8},{8,16},{16,24},{24,0},{1,9},{9,17},{17,25},{25,1},{2,10},{10... | collective-permute-start | bytes 3145736 | tf_op jit(solution)/shard_map/ppermute | solution.py:14
  37.4 1.0 copy-start.2
  38.4 25.4 %collective-permute-start.1 = (bf16[1024,512]{1,0:T(8,128)(2,1)S(1)}, bf16[1024,512]{1,0:T(8,128)(2,1)}, u32[]{:S(2)}, u32[]{:S(2)}) collective-permute-start(bf16[1024,512]{1,0:T(8,128)(2,1)S(1)} %collective-permute-done), channel_id=1, source_target_pairs={{0,8},{8,16},{16,24},{24,0},{1,9},{9,17},{17,25},{25,1},{2,10},{10... | collective-permute-start | bytes 3145736 | tf_op jit(solution)/shard_map/ppermute | solution.py:14
  63.8 24.8 %collective-permute-start.2 = (bf16[1024,512]{1,0:T(8,128)(2,1)}, bf16[1024,512]{1,0:T(8,128)(2,1)}, u32[]{:S(2)}, u32[]{:S(2)}) collective-permute-start(bf16[1024,512]{1,0:T(8,128)(2,1)} %collective-permute-done.1), channel_id=1, source_target_pairs={{0,8},{8,16},{16,24},{24,0},{1,9},{9,17},{17,25},{25,1},{2,10},{10... | collective-permute-start | bytes 3145736 | tf_op jit(solution)/shard_map/ppermute | solution.py:14
  65.1 36.1 %copy-start.3 = (bf16[1024,512]{1,0:T(8,128)(2,1)S(1)}, bf16[1024,512]{1,0:T(8,128)(2,1)}, u32[]{:S(2)}) copy-start(bf16[1024,512]{1,0:T(8,128)(2,1)} %copy-done.2) | copy-start | bytes 3145732
  111.5 1.4 copy-start
Sparse Core Ops, SparseCore 0:
  10.2 84.7 all-gather.1
